TPU v7x, 8 devices: a whole 2x2x1 slice. The times are simulated.
8 devices in a mesh: dp: 2 (over z, y), tp: 4 (over x, core).
Axes of the slice: x: 2, y: 2, z: 1, core: 2. Of those that a mesh axis runs over, the one named last changes fastest.
Arguments:
- x_tokens: bfloat16 [12, 64, 4096], P('dp', 'tp'), parts along dimension 0
- start_pos: int32 [12], P('dp'), parts along dimension 0
- k_cache: bfloat16 [2, 12, 8, 3136, 128], P(None, 'dp', 'tp'), parts along dimension 1
- v_cache: bfloat16 [2, 12, 8, 3136, 128], P(None, 'dp', 'tp'), parts along dimension 1
- w_q: bfloat16 [2, 4096, 6144], P(None, None, 'tp')
- w_k: bfloat16 [2, 4096, 1024], P(None, None, 'tp')
- w_v: bfloat16 [2, 4096, 1024], P(None, None, 'tp')
- w_o: bfloat16 [2, 6144, 4096], P(None, 'tp')
- w_up: bfloat16 [2, 4096, 16384], P(None, None, 'tp')
- w_down: bfloat16 [2, 16384, 4096], P(None, 'tp')
- ln_gain: bfloat16 [2, 2, 4096], replicated
- ln_bias: bfloat16 [2, 2, 4096], replicated
Outputs:
- output 1: bfloat16 [12, 64, 4096], P('dp', 'tp'), parts along dimension 0
- output 2: bfloat16 [2, 12, 8, 3136, 128], P(None, 'dp', 'tp'), parts along dimension 1
- output 3: bfloat16 [2, 12, 8, 3136, 128], P(None, 'dp', 'tp'), parts along dimension 1
There are 2 independent parts. A program takes and returns all parts, laid end to end along the dimension named above; an argument that names none is the same for every part.
All inputs are finite; a program needn't handle non-finite values.
Results may differ from a plain program's by a relative error of at most 0.0189325.
Values are sent between devices in bfloat16 or wider.
A program may use at most 1.25 GiB of HBM per device.

v0:
```python
import functools
import math

import jax
import jax.numpy as jnp
from jax import lax
from jax.experimental import pallas as pl
from jax.experimental.pallas import tpu as pltpu
from jax.sharding import PartitionSpec as P

LN_EPS = 1e-5
ROPE_BASE = 10000.0
NEG_BIG = -1e30
MIN_START = 768
SLOTS = 4
BF = jnp.bfloat16
F32 = jnp.float32


def rope_tables(start, toks, head_dim):
    rot = head_dim // 2
    half = rot // 2
    shape = (toks, head_dim)
    lane = lax.broadcasted_iota(jnp.int32, shape, 1)
    position = start + lax.broadcasted_iota(jnp.int32, shape, 0)
    power = lax.rem(lane, half).astype(F32) * (2.0 / rot)
    angles = position.astype(F32) * jnp.exp(power * -math.log(ROPE_BASE))
    cos_a, sin_a = jnp.cos(angles), jnp.sin(angles)
    upper = jnp.logical_and(lane >= half, lane < rot)
    return jnp.where(lane < rot, cos_a, 1.0), jnp.where(upper, sin_a, 0.0), jnp.where(lane < half, -sin_a, 0.0)


def attn_kernel(layer, dims, start_ref, q_ref, k_ref, v_ref, tab_ref, kc_hbm, vc_hbm, *rest):
    kv, group, toks, hd, s_len, ch = dims
    if layer > 0:
        rest = rest[2:]
    ctx_ref, ko_hbm, vo_hbm, kbuf, vbuf, sbuf, ebuf, qbuf, mbuf, pbuf, lbuf, abuf, in_sem, out_sem = rest
    b = pl.program_id(0)
    nb = pl.num_programs(0) - 1
    s_pad = kbuf.shape[2]
    win = toks + 16
    rows = group * toks
    coef = (hd ** -0.5) * math.log2(math.e)
    slot = lax.rem(b, SLOTS)
    before = lax.rem(b + SLOTS - 1, SLOTS)

    def load(bb):
        sl = lax.rem(bb, SLOTS)
        return [pltpu.make_async_copy(src.at[layer, bb], dst.at[sl, :, pl.ds(0, s_len), :], in_sem.at[sl, i]) for i, (src, dst) in enumerate(((kc_hbm, kbuf), (vc_hbm, vbuf)))]

    def save(bb):
        sl = lax.rem(bb, SLOTS)
        return [pltpu.make_async_copy(src.at[sl, :, pl.ds(0, s_len), :], dst.at[layer, bb], out_sem.at[sl, i]) for i, (src, dst) in enumerate(((kbuf, ko_hbm), (vbuf, vo_hbm)))]

    def run(copies, go):
        for copy in copies:
            copy.start() if go else copy.wait()

    @pl.when(b == 0)
    def _():
        run(load(b), True)
        if s_pad > s_len:
            for sl in range(SLOTS):
                kbuf[sl, :, s_len:, :] = jnp.zeros((kv, s_pad - s_len, hd), BF)
                vbuf[sl, :, s_len:, :] = jnp.zeros((kv, s_pad - s_len, hd), BF)

    @pl.when(b >= 2)
    def _():
        run(save(b - 2), False)

    @pl.when(b == 1)
    def _():
        run(load(b + 1), True)

    start = start_ref[jnp.minimum(b, nb - 1)]
    start_before = start_ref[jnp.maximum(b - 1, 0)]
    half = hd // 4

    def rope(x):
        return x * tab_ref[0, 0] + pltpu.roll(x, half, 1) * tab_ref[1, 0] + pltpu.roll(x, hd - half, 1) * tab_ref[2, 0]

    def patch():
        base = jnp.minimum((start // 16) * 16, s_len - win)
        shift = start - base
        base = pl.multiple_of(base, 16)
        row_id = lax.broadcasted_iota(jnp.int32, (win, hd), 0)
        is_new = jnp.logical_and(row_id >= shift, row_id < shift + toks)
        run(load(b), False)

        @pl.when(b == 0)
        def _():
            run(load(b + 1), True)

        @pl.when(jnp.logical_and(b > 0, b + 2 < nb))
        def _():
            run(load(b + 2), True)

        for h in range(kv):
            cols = slice(h * hd, (h + 1) * hd)
            for buf, fresh in ((kbuf, rope(k_ref[:, cols])), (vbuf, v_ref[:, cols])):
                fresh = fresh.astype(BF).astype(F32)
                fresh = jnp.concatenate([fresh, jnp.zeros((16, hd), F32)], axis=0)
                fresh = pltpu.roll(fresh, shift, 0)
                old = buf[slot, h, pl.ds(base, win), :].astype(F32)
                buf[slot, h, pl.ds(base, win), :] = jnp.where(is_new, fresh, old).astype(BF)
        run(save(b), True)

    step_rows = 64
    blocks = [slice(r, r + step_rows) for r in range(0, ch, step_rows)]

    def chunk(j):
        return pl.ds(pl.multiple_of(j * ch, ch), ch)

    def score(h, j, masked):
        s = lax.dot_general(kbuf[slot, h, chunk(j), :], qbuf[h], (((1,), (1,)), ((), ())), preferred_element_type=F32)
        if masked:
            ahead = lax.broadcasted_iota(jnp.int32, (ch, rows), 0) - lax.rem(lax.broadcasted_iota(jnp.int32, (ch, rows), 1), toks)
            s = jnp.where(ahead <= start - j * ch, s, NEG_BIG)
        sbuf[h] = s

    def scored(h, rb):
        return sbuf[h, rb].reshape(step_rows // 8, 8, rows)

    def peaks(h, peak):
        top = jnp.max(scored(h, blocks[0]), axis=0)
        for rb in blocks[1:]:
            top = jnp.maximum(top, jnp.max(scored(h, rb), axis=0))
        mbuf[h] = peak
        pbuf[h] = jnp.maximum(peak, jnp.max(top, axis=0, keepdims=True))

    def weigh(h):
        peak = pbuf[h]
        alpha = jnp.exp2((mbuf[h] - peak) * coef)
        total = lbuf[h] * alpha
        for rb in blocks:
            e = jnp.exp2((scored(h, rb) - peak) * coef)
            total = total + jnp.sum(e, axis=0)
            ebuf[h, rb] = e.reshape(step_rows, rows).astype(BF)
        return alpha, total

    def mix(h, sl, j, alpha):
        fresh = lax.dot_general(vbuf[sl, h, chunk(j), :], ebuf[h], (((0,), (0,)), ((), ())), preferred_element_type=F32)
        return (abuf[h].reshape(hd // 8, 8, rows) * alpha).reshape(hd, rows) + fresh

    def step(masked_next, j, carry):
        for h in range(kv):
            alpha, lbuf[h] = weigh(h)
            score(h, j + 1, masked_next)
            abuf[h] = mix(h, slot, j, alpha)
        for h in range(kv):
            peaks(h, pbuf[h])
        return carry

    def last_of(bb_start):
        return (bb_start + toks + ch - 1) // ch - 1

    def turn(close, open_next):
        if open_next:
            for h in range(kv):
                for g in range(group):
                    j = h * group + g
                    qbuf[h, g * toks:(g + 1) * toks, :] = rope(q_ref[:, j * hd:(j + 1) * hd]).astype(BF)
            patch()
        for h in range(kv):
            if close:
                alpha, total = weigh(h)
            if open_next:
                score(h, 0, ch > MIN_START)
            if close:
                ctx = (mix(h, before, last_of(start_before), alpha) / jnp.sum(total, axis=0, keepdims=True)).T.astype(BF)
                for g in range(group):
                    j = h * group + g
                    ctx_ref[:, j * hd:(j + 1) * hd] = ctx[g * toks:(g + 1) * toks, :]
        if open_next:
            for h in range(kv):
                peaks(h, jnp.full((8, rows), NEG_BIG, F32))
                lbuf[h] = jnp.zeros((8, rows), F32)
                abuf[h] = jnp.zeros((hd, rows), F32)

    pl.when(b == 0)(functools.partial(turn, False, True))
    pl.when(jnp.logical_and(b > 0, b < nb))(functools.partial(turn, True, True))
    pl.when(b == nb)(functools.partial(turn, True, False))

    @pl.when(b < nb)
    def _():
        n_full = jnp.maximum(start // ch, 1)
        lax.fori_loop(0, n_full - 1, functools.partial(step, False), 0)
        lax.fori_loop(n_full - 1, last_of(start), functools.partial(step, True), 0)

    @pl.when(b == nb)
    def _():
        run(save(b - 1), False)


def attend(layer, qkv, tabs, start_pos, k_cache, v_cache, prev):
    n_seq = start_pos.shape[0]
    _, _, kv, s_len, hd = k_cache.shape
    toks = qkv.shape[0] // n_seq
    kv_width = kv * hd
    q_width = qkv.shape[1] - 2 * kv_width
    group = q_width // kv_width
    n_ch = -(-s_len // 640)
    ch = 128 * -(-s_len // (128 * n_ch))
    rows = group * toks
    dims = (kv, group, toks, hd, s_len, ch)
    any_spec = pl.BlockSpec(memory_space=pl.ANY)
    now = lambda b: jnp.minimum(b, n_seq - 1)
    tab_spec = pl.BlockSpec((3, 1, toks, hd), lambda b, *_: (0, now(b), 0, 0))
    cache_shape = jax.ShapeDtypeStruct(k_cache.shape, BF)
    args = [start_pos, qkv, qkv, qkv, tabs, k_cache, v_cache] + list(prev)
    return pl.pallas_call(
        functools.partial(attn_kernel, layer, dims),
        grid_spec=pltpu.PrefetchScalarGridSpec(
            num_scalar_prefetch=1,
            grid=(n_seq + 1,),
            in_specs=[
                pl.BlockSpec((toks, q_width), lambda b, *_: (now(b), 0)),
                pl.BlockSpec((toks, kv_width), lambda b, *_: (now(b), group)),
                pl.BlockSpec((toks, kv_width), lambda b, *_: (now(b), group + 1)),
                tab_spec,
            ] + [any_spec] * (2 + len(prev)),
            out_specs=[pl.BlockSpec((toks, q_width), lambda b, *_: (jnp.maximum(b - 1, 0), 0)), any_spec, any_spec],
            scratch_shapes=[
                pltpu.VMEM((SLOTS, kv, ch * n_ch, hd), BF),
                pltpu.VMEM((SLOTS, kv, ch * n_ch, hd), BF),
                pltpu.VMEM((kv, ch, rows), F32),
                pltpu.VMEM((kv, ch, rows), BF),
                pltpu.VMEM((kv, rows, hd), BF),
                pltpu.VMEM((kv, 8, rows), F32),
                pltpu.VMEM((kv, 8, rows), F32),
                pltpu.VMEM((kv, 8, rows), F32),
                pltpu.VMEM((kv, hd, rows), F32),
                pltpu.SemaphoreType.DMA((SLOTS, 2)),
                pltpu.SemaphoreType.DMA((SLOTS, 2)),
            ],
        ),
        out_shape=[jax.ShapeDtypeStruct((n_seq * toks, q_width), BF), cache_shape, cache_shape],
        input_output_aliases={7: 1, 8: 2} if prev else {},
        compiler_params=pltpu.CompilerParams(vmem_limit_bytes=60 * 1024 * 1024, dimension_semantics=("arbitrary",)),
        cost_estimate=pl.CostEstimate(flops=8_000_000_000, bytes_accessed=80_000_000, transcendentals=15_000_000),
        name="attend",
    )(*args)


STEPS = 8
WIDE = STEPS + 2


def exchange_kernel(cfg, *args):
    refs = dict(zip(cfg['names'], args))
    n_seq, toks, d_model = cfg['n_seq'], cfg['toks'], cfg['d_model']
    rows = n_seq * toks
    blk = d_model // STEPS
    me = lax.axis_index('tp')
    core = lax.rem(me, 2)
    partner = me + 1 - 2 * core
    counter = lax.rem(me + 2, 4)
    diag = lax.rem(partner + 2, 4)
    order = (me, partner, counter, diag)
    wbuf, xbuf = refs['wbuf'], refs['xbuf']

    barrier = pltpu.get_barrier_semaphore()
    for peer in (partner, counter):
        pl.semaphore_signal(barrier, inc=1, device_id={'tp': peer}, device_id_type=pl.DeviceIdType.MESH)

    def col(n, width=blk):
        return pl.ds(pl.multiple_of(n * width, width), width)

    def remote(src, dst, send, recv, peer):
        return pltpu.make_async_remote_copy(src_ref=src, dst_ref=dst, send_sem=send, recv_sem=recv, device_id={'tp': peer}, device_id_type=pl.DeviceIdType.MESH)

    def fold(values, total):
        for j in range(blk // 128):
            total = total + values[:, j * 128:(j + 1) * 128]
        return total

    def moments(values, state):
        zero = jnp.zeros((rows, 128), F32)
        if state is None:
            state = (jnp.sum(fold(values, zero), axis=-1, keepdims=True) / blk, zero, zero)
        shift, first, second = state
        moved = values - shift
        return shift, fold(moved, first), fold(moved * moved, second)

    def scatter(tag, a_ref, w_copy, slot_of, depth, ahead, late, near_ready=()):
        dsend, drecv, qsend, qrecv, own, part = (refs[k] for k in ('dsend', 'drecv', 'qsend', 'qrecv', 'own', 'part'))
        ds_sem, dr_sem, qs_sem, qr_sem = (refs[tag + k] for k in ('ds', 'dr', 'qs', 'qr'))

        def d_copy(n, i):
            return remote(dsend.at[n, i], drecv.at[n, i], ds_sem.at[n, i], dr_sem.at[n, i], partner)

        def q_copy(n):
            return remote(qsend.at[n], qrecv.at[n], qs_sem.at[n], qr_sem.at[n], counter)

        def step(n, carry):
            @pl.when(n + ahead < STEPS)
            def _():
                w_copy(n + ahead).start()

            w_copy(n).wait()
            cols = col(slot_of(n))
            far = jnp.dot(a_ref[2:4].reshape(2 * rows, depth), wbuf[0:depth, cols], preferred_element_type=F32)
            dsend[n, 0] = far[rows:].astype(BF)
            d_copy(n, 0).start()
            part[...] = far[:rows]
            if near_ready:
                @pl.when(n == 0)
                def _():
                    for copy in near_ready:
                        copy.wait()

            near = jnp.dot(a_ref[0:2].reshape(2 * rows, depth), wbuf[0:depth, cols], preferred_element_type=F32)
            dsend[n, 1] = near[rows:].astype(BF)
            d_copy(n, 1).start()
            own[n] = near[:rows]
            d_copy(n, 0).wait_recv()
            qsend[n] = (part[...] + drecv[n, 0].astype(F32)).astype(BF)
            q_copy(n).start()
            return carry

        half = STEPS - ahead
        lax.fori_loop(0, half, step, 0)
        late(0)
        lax.fori_loop(half, STEPS, step, 0)
        late(1)
        total = None
        for n in range(STEPS):
            cols = slice(n * blk, (n + 1) * blk)
            d_copy(n, 1).wait_recv()
            q_copy(n).wait_recv()
            summed = own[n] + drecv[n, 1].astype(F32) + qrecv[n].astype(F32)
            fresh = (xbuf[:, cols].astype(F32) + summed.astype(BF).astype(F32)).astype(BF)
            xbuf[:, cols] = fresh
            total = moments(fresh.astype(F32), total)
        for n in range(STEPS):
            d_copy(n, 0).wait_send()
            d_copy(n, 1).wait_send()
            q_copy(n).wait_send()
        return total

    def gather(tag, ln_row, total, w_at, n_out, ready, finish):
        near_h, far_h, acc = refs['near_h'], refs['far_h'], refs['acc']
        cs, cr, fs, fr, ps, pr = (refs[tag + k] for k in ('cs', 'cr', 'fs', 'fr', 'ps', 'pr'))
        shift, first, second = total
        offset = jnp.sum(first, axis=-1, keepdims=True) / d_model
        mean = shift + offset
        variance = jnp.maximum(jnp.sum(second, axis=-1, keepdims=True) / d_model - offset * offset, 0.0)
        inv = lax.rsqrt(variance + LN_EPS)

        chunk = blk // 2

        def c_copy(k):
            return remote(near_h.at[pl.ds(0, rows), col(k, chunk)], far_h.at[pl.ds(0, rows), col(k, chunk)], cs.at[k], cr.at[k], counter)

        def f_copy(k):
            return remote(far_h.at[pl.ds(0, rows), col(k, chunk)], far_h.at[pl.ds(rows, rows), col(k, chunk)], fs.at[k], fr.at[k], partner)

        def p_copy(k):
            return remote(near_h.at[pl.ds(0, rows), col(k)], near_h.at[pl.ds(rows, rows), col(k)], ps.at[k], pr.at[k], partner)

        for k in range(STEPS):
            cols = slice(k * blk, (k + 1) * blk)
            gain = refs['ln_gain'][ln_row // 2, ln_row % 2:ln_row % 2 + 1, cols].astype(F32)
            bias = refs['ln_bias'][ln_row // 2, ln_row % 2:ln_row % 2 + 1, cols].astype(F32)
            normed = (xbuf[:, cols].astype(F32) - mean) * inv
            near_h[0:rows, cols] = (normed * (1.0 + gain) + bias).astype(BF)
            if k:
                c_copy(2 * k - 2).start()
                c_copy(2 * k - 1).start()
                p_copy(k - 1).start()
        acc[:, 0:n_out] = jnp.zeros((2 * rows, n_out), F32)
        c_copy(2 * STEPS - 2).start()
        c_copy(2 * STEPS - 1).start()
        p_copy(STEPS - 1).start()
        ready()
        for k in range(STEPS):
            p_copy(k).wait_recv()

        n_blk = n_out // STEPS
        piece = min(1024, n_out)

        def far_dot(k, width, cols):
            return jnp.dot(far_h[:, col(k, width)], wbuf[col(k, width), w_at + cols.start:w_at + cols.stop], preferred_element_type=F32)

        pieces = [slice(n, n + piece) for n in range(0, n_out, piece)]

        def far_step(k, width):
            for cols in pieces:
                acc[:, cols] += far_dot(k, width, cols)

        def pass_on(k):
            c_copy(k).wait_recv()
            f_copy(k).start()

        def near_step(i):
            at = pl.ds(pl.multiple_of(w_at + i * n_blk, n_blk), n_blk)
            finish(0, col(i, n_blk), jnp.dot(near_h[...], wbuf[:, at], preferred_element_type=F32), [i])
            pass_on(2 * i)

        def step(i, carry):
            near_step(i)
            f_copy(2 * i - 2).wait_recv()
            f_copy(2 * i - 1).wait_recv()
            far_step(i - 1, blk)
            pass_on(2 * i + 1)
            return carry

        near_step(0)
        pass_on(1)
        lax.fori_loop(1, STEPS, step, 0)
        f_copy(2 * STEPS - 2).wait_recv()
        far_step(2 * STEPS - 2, chunk)
        f_copy(2 * STEPS - 1).wait_recv()
        for cols in pieces:
            finish(2, cols, acc[:, cols] + far_dot(2 * STEPS - 1, chunk, cols), range(cols.start // n_blk, cols.stop // n_blk))
        for k in range(STEPS):
            p_copy(k).wait_send()
        for k in range(2 * STEPS):
            c_copy(k).wait_send()
            f_copy(k).wait_send()

    def split(value):
        return value.reshape(2, n_seq, toks, value.shape[-1])

    def gather_qkv(layer, total, w_at, start_now):
        stage, y_out = refs['stage'], refs['y_out']
        n_out = y_out.shape[3]
        n_blk = n_out // STEPS

        def y_copy(g, n):
            return pltpu.make_async_copy(stage.at[g, :, :, col(n, n_blk)], y_out.at[:, order[g], :, col(n, n_blk)], refs['y_sem'].at[g, n])

        def ready():
            if start_now:
                tabs = refs['tabs']

                def table(b, carry):
                    for i, part in enumerate(rope_tables(refs['start'][b], tabs.shape[2], tabs.shape[3])):
                        tabs[i, b] = part
                    return carry

                lax.fori_loop(0, n_seq, table, 0)
                tab_copy.start()
            for copy in qkv_copies(layer, w_at):
                copy.wait()

        def finish(g, cols, value, blocks):
            stage[g:g + 2, :, :, cols] = split(value)
            for n in blocks:
                y_copy(g, n).start()
                y_copy(g + 1, n).start()

        if start_now:
            tab_copy = pltpu.make_async_copy(refs['tabs'], refs['tab_out'], refs['tab_sem'])
        gather('g2', 2 * layer, total, w_at, n_out, ready, finish)
        if start_now:
            tab_copy.wait()
        for g in range(4):
            for n in range(STEPS):
                y_copy(g, n).wait()

    def qkv_copies(layer, w_at):
        copies = []
        for i, name in enumerate(('w_q', 'w_k', 'w_v')):
            width = refs[name].shape[2]
            copies.append(pltpu.make_async_copy(refs[name].at[layer], wbuf.at[:, pl.ds(w_at, width)], refs['gw_sem'].at[i]))
            w_at += width
        return copies

    x_copy = pltpu.make_async_copy(refs['x_hbm'], xbuf, refs['x_sem'])
    if cfg['first']:
        x_copy.start()
        x_copy.wait()
        for copy in qkv_copies(0, 0):
            copy.start()
        total = None
        for n in range(STEPS):
            total = moments(xbuf[:, n * blk:(n + 1) * blk].astype(F32), total)
        pl.semaphore_wait(barrier, 2)
        gather_qkv(0, total, 0, True)
        return

    layer = cfg['layer']
    abuf, act = refs['abuf'], refs['act']
    depth = abuf.shape[3]
    a_copies = [pltpu.make_async_copy(refs['a_hbm'].at[:, order[g]], abuf.at[g], refs['a_sem'].at[g]) for g in range(4)]

    def o_copy(n):
        return pltpu.make_async_copy(refs['w_o'].at[layer, :, col(n)], wbuf.at[pl.ds(0, depth), col(n)], refs['ow_sem'].at[n])

    def up_copy(i):
        span = pl.ds(0, depth) if i else pl.ds(depth, d_model - depth)
        return pltpu.make_async_copy(refs['w_up'].at[layer, span, :], wbuf.at[span, pl.ds(0, d_model)], refs['uw_sem'].at[i])

    def down_slot(n):
        return lax.rem(n + STEPS, WIDE)

    def down_copy(n):
        return pltpu.make_async_copy(refs['w_down'].at[layer, :, col(n)], wbuf.at[:, col(down_slot(n))], refs['dw_sem'].at[n])

    for g in (2, 3):
        a_copies[g].start()
    o_copy(0).start()
    for g in (0, 1):
        a_copies[g].start()
    o_copy(1).start()
    o_copy(2).start()
    x_copy.start()
    pl.semaphore_wait(barrier, 2)
    for copy in a_copies[2:]:
        copy.wait()

    def late_up(i):
        up_copy(i).start()
        if i:
            x_copy.wait()

    total = scatter('s1', abuf, o_copy, lambda n: n, depth, 3, late_up, a_copies[:2])

    def ready_up():
        for i in range(2):
            up_copy(i).wait()
        for n in range(WIDE - STEPS):
            down_copy(n).start()

    def finish_up(g, cols, value, blocks):
        act[g:g + 2, :, :, cols] = split(jnp.square(jnp.maximum(value, 0.0)).astype(BF))

    gather('g1', 2 * layer + 1, total, 0, d_model, ready_up, finish_up)

    w_at = (WIDE * blk) - (4 * blk)

    def late_qkv(i):
        if i == 0 and cfg['more']:
            for copy in qkv_copies(layer + 1, w_at):
                copy.start()

    total = scatter('s2', act, down_copy, down_slot, d_model, WIDE - STEPS, late_qkv)
    out_copy = pltpu.make_async_copy(xbuf, refs['x_out'], refs['x_sem'])
    out_copy.start()
    if cfg['more']:
        gather_qkv(layer + 1, total, w_at, False)
    out_copy.wait()


def exchange(cid, x, ln_gain, ln_bias, qkv_weights, *, n_seq, layer=-1, more=True, a=None, weights=(), start_pos=None, head_dim=0):
    rows, d_model = x.shape
    toks = rows // n_seq
    blk = d_model // STEPS
    first = a is None
    any_spec, vmem = pl.BlockSpec(memory_space=pl.ANY), pl.BlockSpec(memory_space=pltpu.VMEM)
    dma = pltpu.SemaphoreType.DMA
    ins = [('x_hbm', x, any_spec), ('ln_gain', ln_gain, vmem), ('ln_bias', ln_bias, vmem)]
    outs = []
    qkv_out = sum(w.shape[2] for w in qkv_weights)
    width = qkv_out if first else WIDE * blk
    scr = [('wbuf', pltpu.VMEM((d_model, width), BF)), ('xbuf', pltpu.VMEM((rows, d_model), BF)), ('x_sem', dma)]
    scr += [
        ('near_h', pltpu.VMEM((2 * rows, d_model), BF)), ('far_h', pltpu.VMEM((2 * rows, d_model), BF)),
        ('acc', pltpu.VMEM((2 * rows, qkv_out if first else d_model), F32)),
    ]
    gather_tags, flops, moved = [], 0, 4_000_000
    if not first:
        w_o, w_up, w_down = weights
        depth = a.shape[3]
        ins += [('a_hbm', a, any_spec), ('w_o', w_o, any_spec), ('w_up', w_up, any_spec), ('w_down', w_down, any_spec)]
        outs += [('x_out', jax.ShapeDtypeStruct(x.shape, BF))]
        scr += [
            ('abuf', pltpu.VMEM((4, n_seq, toks, depth), BF)), ('act', pltpu.VMEM((4, n_seq, toks, d_model), BF)),
            ('dsend', pltpu.VMEM((STEPS, 2, rows, blk), BF)), ('drecv', pltpu.VMEM((STEPS, 2, rows, blk), BF)),
            ('qsend', pltpu.VMEM((STEPS, rows, blk), BF)), ('qrecv', pltpu.VMEM((STEPS, rows, blk), BF)),
            ('own', pltpu.VMEM((STEPS, rows, blk), F32)), ('part', pltpu.VMEM((rows, blk), F32)),
            ('a_sem', dma((4,))), ('ow_sem', dma((STEPS,))), ('uw_sem', dma((2,))), ('dw_sem', dma((STEPS,))),
        ]
        for tag in ('s1', 's2'):
            scr += [(tag + k, dma((STEPS, 2))) for k in ('ds', 'dr')] + [(tag + k, dma((STEPS,))) for k in ('qs', 'qr')]
        gather_tags.append('g1')
        flops += 2 * 4 * rows * d_model * (depth + 2 * d_model)
        moved += 2 * d_model * (depth + 2 * d_model)
    if more:
        ins += list(zip(('w_q', 'w_k', 'w_v'), qkv_weights, [any_spec] * 3))
        outs += [('y_out', jax.ShapeDtypeStruct((n_seq, 4, toks, qkv_out), F32))]
        scr += [('stage', pltpu.VMEM((4, n_seq, toks, qkv_out), F32)), ('gw_sem', dma((3,))), ('y_sem', dma((4, STEPS)))]
        gather_tags.append('g2')
        flops += 2 * 4 * rows * d_model * qkv_out
        moved += 2 * d_model * qkv_out
    if first:
        tab_shape = (3, n_seq, 4 * toks, head_dim)
        ins += [('start', start_pos, pl.BlockSpec(memory_space=pltpu.SMEM))]
        outs += [('tab_out', jax.ShapeDtypeStruct(tab_shape, F32))]
        scr += [('tabs', pltpu.VMEM(tab_shape, F32)), ('tab_sem', dma)]
    for tag in gather_tags:
        scr += [(tag + k, dma((2 * STEPS,))) for k in ('cs', 'cr', 'fs', 'fr')] + [(tag + k, dma((STEPS,))) for k in ('ps', 'pr')]
    cfg = dict(names=[i[0] for i in ins] + [o[0] for o in outs] + [s[0] for s in scr], layer=layer, first=first, more=more, n_seq=n_seq, toks=toks, d_model=d_model)
    return pl.pallas_call(
        functools.partial(exchange_kernel, cfg),
        in_specs=[i[2] for i in ins],
        out_specs=[any_spec] * len(outs),
        out_shape=[o[1] for o in outs],
        scratch_shapes=[s[1] for s in scr],
        compiler_params=pltpu.CompilerParams(collective_id=cid, has_side_effects=True, vmem_limit_bytes=67_000_000),
        cost_estimate=pl.CostEstimate(flops=flops, bytes_accessed=moved, transcendentals=0),
        name='gather_first' if first else 'block' if more else 'block_last',
    )(*[i[1] for i in ins])


def solution(mesh):
    tok_spec = P('dp', 'tp', None)
    cache_spec = P(None, 'dp', 'tp', None, None)
    col_spec = P(None, None, 'tp')
    row_spec = P(None, 'tp', None)

    def device_fn(x_loc, start_pos, k_cache, v_cache, w_q, w_k, w_v, w_o, w_up, w_down, ln_gain, ln_bias):
        n_layers = w_q.shape[0]
        n_seq, tok_loc, d_model = x_loc.shape
        new_len = tok_loc * 4
        rows = n_seq * new_len
        hidden = x_loc.reshape(n_seq * tok_loc, d_model)
        prev = ()
        qkv_weights = (w_q, w_k, w_v)
        qkv, tabs = exchange(0, hidden, ln_gain, ln_bias, qkv_weights, n_seq=n_seq, start_pos=start_pos, head_dim=k_cache.shape[4])
        for layer in range(n_layers):
            context, *prev = attend(layer, qkv.reshape(rows, -1), tabs, start_pos, k_cache, v_cache, prev)
            context = context.reshape(n_seq, 4, tok_loc, -1)
            outs = exchange(layer + 1, hidden, ln_gain, ln_bias, qkv_weights, n_seq=n_seq, layer=layer, more=layer + 1 < n_layers, a=context, weights=(w_o, w_up, w_down))
            hidden, qkv = outs if layer + 1 < n_layers else (outs[0], None)
        return hidden.reshape(x_loc.shape), prev[0], prev[1]

    return jax.shard_map(device_fn, mesh=mesh, in_specs=(tok_spec, P('dp'), cache_spec, cache_spec, col_spec, col_spec, col_spec, row_spec, col_spec, row_spec, P(), P()), out_specs=(tok_spec, cache_spec, cache_spec), check_vma=False)
```

profile of v0, /device:TPU:0, one launch (start us, length us, event | category | flops | bytes accessed | tf_op | source)
XLA Modules:
  0.0 243.0 jit_solution(11700802385102687848)
XLA Ops:
  0.6 27.6 %gather_first.1 = (f32[6,4,16,2048]{3,2,1,0:T(8,128)}, f32[3,6,64,128]{3,2,1,0:T(8,128)}) custom-call(bf16[96,4096]{1,0:T(8,128)(2,1)} %bitcast.13, bf16[2,2,4096]{2,1,0:T(2,128)(2,1)} %args_1_.8, bf16[2,2,4096]{2,1,0:T(2,128)(2,1)} %args_2_.8, bf16[2,4096,1536]{2,1,0:T(8,128)(2,1)} %args_7_.4, bf16[2,4096,256]{2,1,0:T(8,128)(2,1)} %args_8_.4, ...), custom_call_target="tpu_custom_call" | custom-call | flops 6442450944 | bytes 20777216 | tf_op jit(solution)/shard_map/gather_first/pallas_call | solution.py:595
  28.2 27.0 %attend.2 = (bf16[384,1536]{1,0:T(8,128)(2,1)}, bf16[2,6,2,3136,128]{4,3,2,1,0:T(8,128)(2,1)}, bf16[2,6,2,3136,128]{4,3,2,1,0:T(8,128)(2,1)}) custom-call(s32[6]{0:T(128)} %start_ref.3, f32[384,2048]{1,0:T(8,128)} %bitcast.9, f32[384,2048]{1,0:T(8,128)} %bitcast.10, f32[384,2048]{1,0:T(8,128)} %bitcast.11, f32[3,6,64,128]{3,2,1,0:T(8,128)} %get-tuple-element.14.tab_ref, ...), custom_call_target="tpu_custom_call" | custom-call | flops 8000000000 | bytes 80000000 | tf_op jit(solution)/shard_map/attend/pallas_call | solution.py:211
  55.2 89.9 %block.1 = (bf16[96,4096]{1,0:T(8,128)(2,1)}, f32[6,4,16,2048]{3,2,1,0:T(8,128)}) custom-call(bf16[96,4096]{1,0:T(8,128)(2,1)} %bitcast.14, bf16[2,2,4096]{2,1,0:T(2,128)(2,1)} %args_1_.8, bf16[2,2,4096]{2,1,0:T(2,128)(2,1)} %args_2_.8, bf16[6,4,16,1536]{3,2,1,0:T(8,128)(2,1)} %bitcast.15, bf16[2,1536,4096]{2,1,0:T(8,128)(2,1)} %args_4_.8, ...), custom_call_target="tpu_custom_call" | custom-call | flops 37044092928 | bytes 100468992 | tf_op jit(solution)/shard_map/block/pallas_call | solution.py:595
  145.1 27.2 %attend.3 = (bf16[384,1536]{1,0:T(8,128)(2,1)}, bf16[2,6,2,3136,128]{4,3,2,1,0:T(8,128)(2,1)}, bf16[2,6,2,3136,128]{4,3,2,1,0:T(8,128)(2,1)}) custom-call(s32[6]{0:T(128)} %start_ref.3, f32[384,2048]{1,0:T(8,128)} %bitcast.6, f32[384,2048]{1,0:T(8,128)} %bitcast.7, f32[384,2048]{1,0:T(8,128)} %bitcast.8, ...), custom_call_target="tpu_custom_call", output_to_operand_aliasing={{1}: (7, {}), {2}: (8, {})} | custom-call | flops 8000000000 | bytes 80000000 | tf_op jit(solution)/shard_map/attend/pallas_call | solution.py:211
  172.4 68.6 %block_last.1 = bf16[96,4096]{1,0:T(8,128)(2,1)} custom-call(bf16[96,4096]{1,0:T(8,128)(2,1)} %get-tuple-element.16.args_0_, bf16[2,2,4096]{2,1,0:T(2,128)(2,1)} %args_1_.8, bf16[2,2,4096]{2,1,0:T(2,128)(2,1)} %args_2_.8, bf16[6,4,16,1536]{3,2,1,0:T(8,128)(2,1)} %bitcast.16, bf16[2,1536,4096]{2,1,0:T(8,128)(2,1)} %args_4_.8, bf16[2,4096,4096]{2,1,0:T(8,128)(2,1)} %args_5_.8, ...), custom_call_target="tpu_custom_call" | custom-call | flops 30601641984 | bytes 83691776 | tf_op jit(solution)/shard_map/block_last/pallas_call | solution.py:595
  241.0 2.1 copy.20
where the time goes:
time: 241 us; the launch traced here: 243 us
  Pallas kernels  240 us (100%)
    pallas_call x3, Pallas kernels, exchange(): pl.pallas_call(functools.partial(exchange_kernel, cfg), in_specs=[i[2] fo...  186 us
    pallas_call x2, Pallas kernels, attend(): pl.pallas_call(functools.partial(attn_kernel, layer, dims), grid_spec=plt...  54.2 us

commit v1 on v0

--- a/solution.py
+++ b/solution.py
@@ -68,9 +68,9 @@
     def _():
         run(save(b - 2), False)
 
-    @pl.when(b == 1)
+    @pl.when(jnp.logical_and(b > 0, b + 2 < nb))
     def _():
-        run(load(b + 1), True)
+        run(load(b + 2), True)
 
     start = start_ref[jnp.minimum(b, nb - 1)]
     start_before = start_ref[jnp.maximum(b - 1, 0)]
@@ -90,9 +90,6 @@
         @pl.when(b == 0)
         def _():
             run(load(b + 1), True)
-
-        @pl.when(jnp.logical_and(b > 0, b + 2 < nb))
-        def _():
             run(load(b + 2), True)
 
         for h in range(kv):

time: 241 us -> 239 us (level); the launches traced: 243 us -> 235 us
  Pallas kernels: 240 us -> 233 us
    pallas_call x2, Pallas kernels: 54.2 us -> 46.5 us  [attend(): pl.pallas_call(functools.partial(attn_kernel, layer, dims), grid_spec=plt...]
where the time goes in v1:
time: 239 us; the launch traced here: 235 us
  Pallas kernels  233 us (97%)
    pallas_call x3, Pallas kernels, exchange(): pl.pallas_call(functools.partial(exchange_kernel, cfg), in_specs=[i[2] fo...  186 us
    pallas_call x2, Pallas kernels, attend(): pl.pallas_call(functools.partial(attn_kernel, layer, dims), grid_spec=plt...  46.5 us

profile of v1, /device:TPU:0, one launch (start us, length us, event | category | flops | bytes accessed | tf_op | source)
XLA Modules:
  0.0 235.3 jit_solution(8753093771431778602)
XLA Ops:
  0.6 27.6 %gather_first.1 = (f32[6,4,16,2048]{3,2,1,0:T(8,128)}, f32[3,6,64,128]{3,2,1,0:T(8,128)}) custom-call(bf16[96,4096]{1,0:T(8,128)(2,1)} %bitcast.13, bf16[2,2,4096]{2,1,0:T(2,128)(2,1)} %args_1_.8, bf16[2,2,4096]{2,1,0:T(2,128)(2,1)} %args_2_.8, bf16[2,4096,1536]{2,1,0:T(8,128)(2,1)} %args_7_.4, bf16[2,4096,256]{2,1,0:T(8,128)(2,1)} %args_8_.4, ...), custom_call_target="tpu_custom_call" | custom-call | flops 6442450944 | bytes 20777216 | tf_op jit(solution)/shard_map/gather_first/pallas_call | solution.py:592
  28.2 23.1 %attend.2 = (bf16[384,1536]{1,0:T(8,128)(2,1)}, bf16[2,6,2,3136,128]{4,3,2,1,0:T(8,128)(2,1)}, bf16[2,6,2,3136,128]{4,3,2,1,0:T(8,128)(2,1)}) custom-call(s32[6]{0:T(128)} %start_ref.3, f32[384,2048]{1,0:T(8,128)} %bitcast.9, f32[384,2048]{1,0:T(8,128)} %bitcast.10, f32[384,2048]{1,0:T(8,128)} %bitcast.11, f32[3,6,64,128]{3,2,1,0:T(8,128)} %get-tuple-element.14.tab_ref, ...), custom_call_target="tpu_custom_call" | custom-call | flops 8000000000 | bytes 80000000 | tf_op jit(solution)/shard_map/attend/pallas_call | solution.py:208
  51.3 90.0 %block.1 = (bf16[96,4096]{1,0:T(8,128)(2,1)}, f32[6,4,16,2048]{3,2,1,0:T(8,128)}) custom-call(bf16[96,4096]{1,0:T(8,128)(2,1)} %bitcast.14, bf16[2,2,4096]{2,1,0:T(2,128)(2,1)} %args_1_.8, bf16[2,2,4096]{2,1,0:T(2,128)(2,1)} %args_2_.8, bf16[6,4,16,1536]{3,2,1,0:T(8,128)(2,1)} %bitcast.15, bf16[2,1536,4096]{2,1,0:T(8,128)(2,1)} %args_4_.8, ...), custom_call_target="tpu_custom_call" | custom-call | flops 37044092928 | bytes 100468992 | tf_op jit(solution)/shard_map/block/pallas_call | solution.py:592
  141.3 23.4 %attend.3 = (bf16[384,1536]{1,0:T(8,128)(2,1)}, bf16[2,6,2,3136,128]{4,3,2,1,0:T(8,128)(2,1)}, bf16[2,6,2,3136,128]{4,3,2,1,0:T(8,128)(2,1)}) custom-call(s32[6]{0:T(128)} %start_ref.3, f32[384,2048]{1,0:T(8,128)} %bitcast.6, f32[384,2048]{1,0:T(8,128)} %bitcast.7, f32[384,2048]{1,0:T(8,128)} %bitcast.8, ...), custom_call_target="tpu_custom_call", output_to_operand_aliasing={{1}: (7, {}), {2}: (8, {})} | custom-call | flops 8000000000 | bytes 80000000 | tf_op jit(solution)/shard_map/attend/pallas_call | solution.py:208
  164.7 68.6 %block_last.1 = bf16[96,4096]{1,0:T(8,128)(2,1)} custom-call(bf16[96,4096]{1,0:T(8,128)(2,1)} %get-tuple-element.16.args_0_, bf16[2,2,4096]{2,1,0:T(2,128)(2,1)} %args_1_.8, bf16[2,2,4096]{2,1,0:T(2,128)(2,1)} %args_2_.8, bf16[6,4,16,1536]{3,2,1,0:T(8,128)(2,1)} %bitcast.16, bf16[2,1536,4096]{2,1,0:T(8,128)(2,1)} %args_4_.8, bf16[2,4096,4096]{2,1,0:T(8,128)(2,1)} %args_5_.8, ...), custom_call_target="tpu_custom_call" | custom-call | flops 30601641984 | bytes 83691776 | tf_op jit(solution)/shard_map/block_last/pallas_call | solution.py:592
  233.2 2.1 copy.20
